TPU v7x, 512 devices: a whole 4x4x16 slice. The times are simulated.
512 devices in a mesh: dp: 8 (over y, x_lo), seq: 64 (over x_hi, z, core).
Axes of the slice: x: 4 (x_hi: 2, x_lo: 2; x = x_hi * 2 + x_lo), y: 4, z: 16, core: 2. Of those that a mesh axis runs over, the one named last changes fastest.
Arguments:
- hidden_in: bfloat16 [8, 4096, 2048], P('dp', 'seq'), may hold values from -6 to 6
- attn_gain: float32 [2048], replicated, may hold values from 0.1 to 1.9
- w_query: bfloat16 [2048, 1280], P('dp'), may hold values from -2 to 2
- w_keyval: bfloat16 [2048, 512], P('dp'), may hold values from -1 to 1
- w_output: bfloat16 [1280, 2048], P(None, 'dp'), may hold values from -0.15625 to 0.15625
- post_gain: float32 [2048], replicated, may hold values from 0.1 to 1.9
Outputs:
- hidden_out: bfloat16 [8, 4096, 2048], P('dp', 'seq')
All inputs are finite; a program needn't handle non-finite values.
Results may differ from a plain program's by a relative error of at most 0.009.
Values may be sent and summed in bfloat16 or wider, within the bound.
A program may use at most 64 MiB of HBM per device.

v0:
```python
import jax
import jax.numpy as jnp
from jax import lax
from jax.sharding import Mesh
from jax.sharding import PartitionSpec as P

SEQ = ("seq_0", "seq_1", "seq_2")


def split_up(array, dim, peers):
    before, after = (array.shape[:dim], array.shape[dim + 1 :])
    return jnp.moveaxis(array.reshape(*before, peers, -1, *after), dim, 0)


def sum_at_owner(array, axis, dim):
    blocks = split_up(array, dim, lax.axis_size(axis))
    arrived = lax.all_to_all(blocks, axis, split_axis=0, concat_axis=0, tiled=True)
    return arrived.sum(axis=0)


def from_everyone(array, axis):
    copies = jnp.broadcast_to(array, (lax.axis_size(axis), *array.shape))
    return lax.all_to_all(copies, axis, split_axis=0, concat_axis=0, tiled=True)


def joined_along(blocks, dim):
    shape = list(blocks.shape[1:])
    shape[dim] *= blocks.shape[0]
    return jnp.moveaxis(blocks, 0, dim).reshape(shape)


def whole_of(array, axes, dim):
    far, near = axes
    blocks = from_everyone(from_everyone(array, far), near)
    return joined_along(blocks.swapaxes(0, 1).reshape(-1, *array.shape), dim)


def side_by_side(arrays, axis, dim, along):
    both = jnp.concatenate(arrays, axis=along)
    filled, at, finished = (whole_of(both, axis, dim), 0, [])
    for a in arrays:
        finished.append(lax.slice_in_dim(filled, at, at + a.shape[along], axis=along))
        at += a.shape[along]
    return tuple(finished)


def collect(array, axis, dim):
    blocks = from_everyone(array, axis)
    return joined_along(blocks, dim)


def rms_norm(v, gain):
    v = v.astype(jnp.float32)
    return v * lax.rsqrt(jnp.mean(v * v, axis=-1, keepdims=True) + 1e-06) * gain


def rotary(t, positions):
    half = t.shape[-1] // 2
    freq = jnp.exp(-jnp.log(10000.0) * jnp.arange(half, dtype=jnp.float32) * 2.0 / t.shape[-1])
    angle = positions.astype(jnp.float32)[:, None, None] * freq[None, None, :]
    cosine = jnp.cos(angle)
    sine = jnp.sin(angle)
    first = t[..., :half]
    second = t[..., half:]
    return jnp.concatenate(
        [first * cosine - second * sine, second * cosine + first * sine], axis=-1
    )


def local(hidden_in, attn_gain, w_query, w_keyval, w_output, post_gain):
    frame = hidden_in[0]
    count = frame.shape[0]
    head_dim = w_keyval.shape[1] // 2
    width_q = w_query.shape[1]
    num_heads = width_q // head_dim
    normed = rms_norm(frame, attn_gain).astype(jnp.bfloat16)
    slices = lax.all_to_all(normed, "dp", split_axis=1, concat_axis=0, tiled=True)
    joined = jnp.concatenate([w_query, w_keyval], axis=1)
    summed = sum_at_owner(jnp.dot(slices, joined, preferred_element_type=jnp.float32), "dp", 0)
    query_raw = summed[:, :width_q]
    keyval_raw = summed[:, width_q:]
    positions = lax.axis_index(SEQ) * count + jnp.arange(count, dtype=jnp.int32)
    query = (
        rotary(query_raw.reshape(count, num_heads, head_dim), positions) * head_dim ** (-0.5)
    ).astype(jnp.bfloat16)
    keys = rotary(keyval_raw[:, None, :head_dim], positions)[:, 0, :].astype(jnp.bfloat16)
    values = keyval_raw[:, head_dim:].astype(jnp.bfloat16)
    stacked = jnp.transpose(query, (1, 0, 2)).reshape(num_heads * count, head_dim)
    rows_all = num_heads * count
    running_max = jnp.full((rows_all,), -1e30, jnp.float32)
    key_piece, value_piece = side_by_side((keys, values), (("seq_0", "seq_1"), "seq_2"), 0, 1)
    scores = lax.dot_general(
        stacked, key_piece, (((1,), (1,)), ((), ())), preferred_element_type=jnp.float32
    )
    new_max = jnp.maximum(running_max, jnp.max(scores, axis=1))
    expo = jnp.exp(scores - new_max[:, None])
    new_total = jnp.sum(expo, axis=1)
    new_sum = jnp.dot(expo.astype(jnp.bfloat16), value_piece, preferred_element_type=jnp.float32)
    heads = (new_sum / new_total[:, None]).reshape(num_heads, count, head_dim)
    attended = jnp.transpose(heads, (1, 0, 2)).reshape(count, width_q).astype(jnp.bfloat16)
    episode_parts = jnp.dot(
        collect(attended, "dp", 0), w_output, preferred_element_type=jnp.float32
    )
    projected = lax.all_to_all(
        episode_parts.astype(jnp.bfloat16), "dp", split_axis=0, concat_axis=1, tiled=True
    ).astype(episode_parts.dtype)
    result = frame.astype(jnp.float32) + rms_norm(projected, post_gain)
    return result.astype(jnp.bfloat16)[None]


def solution(mesh):
    split = Mesh(
        mesh.devices.reshape(mesh.shape["dp"], 2, 16, 2), ("dp", "seq_0", "seq_1", "seq_2")
    )
    return jax.shard_map(
        local,
        mesh=split,
        in_specs=(P("dp", SEQ, None), P(), P("dp", None), P("dp", None), P(None, "dp"), P()),
        out_specs=P("dp", SEQ, None),
        check_vma=False,
    )
```

profile of v0, /device:TPU:32, one launch (start us, length us, event | category | flops | bytes accessed | tf_op | source)
XLA Modules:
  0.0 233.7 jit_solution(17389316271846565419)
XLA Ops:
  0.0 1.2 multiply_reduce_fusion
  1.2 0.7 mul.162
  1.9 1.0 copy.17
  3.1 12.5 %all_to_all.46 = bf16[64,8,256]{2,0,1:T(8,128)(2,1)S(1)} all-to-all(bf16[64,8,256]{2,0,1:T(8,128)(2,1)S(1)} %fusion.24), channel_id=1, replica_groups=mesh['dp'=8,'seq_0'=2,'seq_1'=16,'seq_2'=2] {'dp'}, dimensions={1} | all-to-all | bytes 524288 | tf_op jit(solution)/shard_map/all_to_all | solution.py:77
  15.6 3.7 %fusion.18 = f32[8,64,1792]{2,1,0:T(8,128)} fusion(bf16[256,512]{1,0:T(8,128)(2,1)} %param.9, bf16[256,1280]{1,0:T(8,128)(2,1)} %param.8, bf16[64,8,256]{2,0,1:T(8,128)(2,1)S(1)} %all_to_all.46), kind=kOutput, calls=%fused_computation.12 | convolution fusion | flops 471597056 | bytes 4849664 | tf_op jit(solution)/shard_map/dot_general | solution.py:79
  19.3 4.5 %all-to-all-start.1 = ((f32[8,64,1792]{2,1,0:T(8,128)}), f32[8,64,1792]{2,1,0:T(8,128)}, u32[]{:S(2)}, u32[]{:S(2)}) async-start(f32[8,64,1792]{2,1,0:T(8,128)} %fusion.18), calls=%async_computation.1 | async-start | bytes 7340032 | tf_op jit(solution)/shard_map/all_to_all | solution.py:17
  23.8 42.7 %all-to-all-done.1 = f32[8,64,1792]{2,1,0:T(8,128)} async-done(((f32[8,64,1792]{2,1,0:T(8,128)}), f32[8,64,1792]{2,1,0:T(8,128)}, u32[]{:S(2)}, u32[]{:S(2)}) %all-to-all-start.1) | async-done | bytes 3670048 | tf_op jit(solution)/shard_map/all_to_all | solution.py:17
  66.5 2.3 reduce_sum.37
  69.1 1.6 broadcast_in_dim.11
  70.7 17.5 %all-to-all-start.2 = ((bf16[32,64,512]{2,1,0:T(8,128)(2,1)}), bf16[32,64,512]{2,1,0:T(8,128)(2,1)S(1)}, u32[]{:S(2)}, u32[]{:S(2)}) async-start(bf16[32,64,512]{2,1,0:T(8,128)(2,1)} %broadcast_in_dim.11), calls=%async_computation.2 | async-start | bytes 4194304 | tf_op jit(solution)/shard_map/all_to_all | solution.py:23
  88.4 0.8 slice.40
  89.2 1.1 reshape.232
  90.4 95.7 %all-to-all-done.2 = bf16[32,64,512]{2,1,0:T(8,128)(2,1)S(1)} async-done(((bf16[32,64,512]{2,1,0:T(8,128)(2,1)}), bf16[32,64,512]{2,1,0:T(8,128)(2,1)S(1)}, u32[]{:S(2)}, u32[]{:S(2)}) %all-to-all-start.2) | async-done | bytes 2097184 | tf_op jit(solution)/shard_map/all_to_all | solution.py:23
  186.1 0.5 broadcast_in_dim.12
  186.6 7.1 %all_to_all.47 = bf16[2,32,64,512]{3,2,1,0:T(8,128)(2,1)S(1)} all-to-all(bf16[2,32,64,512]{3,2,1,0:T(8,128)(2,1)S(1)} %broadcast_in_dim.12), channel_id=1, replica_groups=mesh['dp'=8,'seq_0'=2,'seq_1'=16,'seq_2'=2] {'seq_2'}, dimensions={0} | all-to-all | bytes 8388608 | tf_op jit(solution)/shard_map/all_to_all | solution.py:23
  193.7 0.5 copy.14
  194.2 1.0 fusion.36
  195.2 0.9 fusion
  196.1 0.9 fusion.13
  197.1 24.8 %all_to_all.48 = bf16[8,64,1280]{2,1,0:T(8,128)(2,1)S(1)} all-to-all(bf16[8,64,1280]{2,1,0:T(8,128)(2,1)S(1)} %broadcast_in_dim.14), channel_id=1, replica_groups=mesh['dp'=8,'seq_0'=2,'seq_1'=16,'seq_2'=2] {'dp'}, dimensions={0} | all-to-all | bytes 2621440 | tf_op jit(solution)/shard_map/all_to_all | solution.py:23
  221.9 0.5 convolution_convert_fusion
  222.4 9.8 %all_to_all.49 = bf16[8,64,256]{2,1,0:T(8,128)(2,1)S(1)} all-to-all(bf16[8,64,256]{2,1,0:T(8,128)(2,1)S(1)} %bitcast.40), channel_id=1, replica_groups=mesh['dp'=8,'seq_0'=2,'seq_1'=16,'seq_2'=2] {'dp'}, dimensions={0} | all-to-all | bytes 524288 | tf_op jit(solution)/shard_map/all_to_all | solution.py:104
  232.4 0.3 copy.16
  232.8 0.9 add_convert_fusion
  (26 shorter events, 1.2 us)
Async XLA Ops:
  0.0 221.9 %copy-start = (bf16[1280,256]{1,0:T(8,128)(2,1)S(1)}, bf16[1280,256]{1,0:T(8,128)(2,1)}, u32[]{:S(2)}) copy-start(bf16[1280,256]{1,0:T(8,128)(2,1)} %param.10) | copy-start | bytes 1966084
  19.3 47.3 %all-to-all-start.1 = ((f32[8,64,1792]{2,1,0:T(8,128)}), f32[8,64,1792]{2,1,0:T(8,128)}, u32[]{:S(2)}, u32[]{:S(2)}) async-start(f32[8,64,1792]{2,1,0:T(8,128)} %fusion.18), calls=%async_computation.1 | async-start | bytes 7340032 | tf_op jit(solution)/shard_map/all_to_all | solution.py:17
  70.7 115.4 %all-to-all-start.2 = ((bf16[32,64,512]{2,1,0:T(8,128)(2,1)}), bf16[32,64,512]{2,1,0:T(8,128)(2,1)S(1)}, u32[]{:S(2)}, u32[]{:S(2)}) async-start(bf16[32,64,512]{2,1,0:T(8,128)(2,1)} %broadcast_in_dim.11), calls=%async_computation.2 | async-start | bytes 4194304 | tf_op jit(solution)/shard_map/all_to_all | solution.py:23
  221.9 11.0 %copy-start.1 = (bf16[1,64,2048]{2,1,0:T(8,128)(2,1)S(1)}, bf16[1,64,2048]{2,1,0:T(8,128)(2,1)}, u32[]{:S(2)}) copy-start(bf16[1,64,2048]{2,1,0:T(8,128)(2,1)} %param.6) | copy-start | bytes 786436
  221.9 11.0 %copy-start.2 = (f32[2048]{0:T(1024)S(1)}, f32[2048]{0:T(1024)}, u32[]{:S(2)}) copy-start(f32[2048]{0:T(1024)} %param.11) | copy-start | bytes 24580
where the time goes:
time: 234 us
  waiting for transfers between devices  138 us (59%)
  blocking collectives  54.2 us (23%)
  starting transfers between devices  22 us (9%)
  local copies, waits for them, and re-layouts  6.72 us (3%)
  other arithmetic  6.15 us (3%)
  matrix products  6.05 us (3%)
    all_to_all x1, waiting for transfers between devices, from_everyone(): return lax.all_to_all(copies, axis, split_axis=0, concat_axis=0, tiled=True)  95.7 us
    all_to_all x1, waiting for transfers between devices, sum_at_owner(): lax.all_to_all(blocks, axis, split_axis=0, concat_axis=0, tiled=True)  42.7 us
    all_to_all x2, blocking collectives, from_everyone(): return lax.all_to_all(copies, axis, split_axis=0, concat_axis=0, tiled=True)  31.9 us
    all_to_all x1, starting transfers between devices, from_everyone(): return lax.all_to_all(copies, axis, split_axis=0, concat_axis=0, tiled=True)  17.5 us
    all_to_all x1, blocking collectives, local(): lax.all_to_all(normed, 'dp', split_axis=1, concat_axis=0, tiled=True)  12.5 us
    all_to_all x1, blocking collectives, local(): lax.all_to_all(episode_parts.astype(jnp.bfloat16), 'dp', split_axis=0, co...  9.82 us
  transfers between devices with their start and end apart: 2, of which 2 were waited for; matrix products, arithmetic and copies ran while one was open for 1% of the time, Pallas kernels for 0%

commit v1 on v0

v1 whole, which is shorter than its diff:
```python
import functools

import jax
import jax.numpy as jnp
from jax import lax
from jax.experimental import pallas as pl
from jax.experimental.pallas import tpu as pltpu
from jax.sharding import PartitionSpec as P

BF16 = jnp.bfloat16
F32 = jnp.float32

ROWS = 64
HD = 256
HEADS = 5
NCH = 2 + HEADS + HEADS
NZ = 16
HALF = NZ // 2


def ring_kernel(
    hid, gain, cos, sin, pgain, wq, wkv, wo, out,
    wbuf, kvbuf, nrel, qbuf, acc, mrow, lrow, proj,
    lsem, wss, wrs, kss, krs, css, crs,
):
    dp = lax.axis_index("dp")
    sq = lax.axis_index("seq")
    y, xl = dp // 2, dp % 2
    xh, z, c = sq // 32, (sq // 2) % NZ, sq % 2

    def dev(yy, xll, xhh, zz, cc):
        return (yy * 2 + xll, xhh * 32 + zz * 2 + cc)

    yp = dev((y + 1) % 4, xl, xh, z, c)
    ym = dev((y + 3) % 4, xl, xh, z, c)
    xp = dev(y, 1 - xl, (xh + xl) % 2, z, c)
    xm = dev(y, 1 - xl, (xh + 1 - xl) % 2, z, c)
    xo = dev(y, xl, 1 - xh, z, c)
    zp = dev(y, xl, xh, (z + 1) % NZ, c)
    zm = dev(y, xl, xh, (z + NZ - 1) % NZ, c)
    co = dev(y, xl, xh, z, 1 - c)

    def load(ch):
        if ch < 2:
            src = wkv.at[:, pl.ds(ch * HD, HD)]
        elif ch < 2 + HEADS:
            src = wq.at[:, pl.ds((ch - 2) * HD, HD)]
        else:
            src = wo.at[pl.ds((ch - 2 - HEADS) * HD, HD), :]
        return pltpu.make_async_copy(src, wbuf.at[ch, 0], lsem.at[ch])

    for ch in range(NCH):
        load(ch).start()

    barrier = pltpu.get_barrier_semaphore()
    for peer in (yp, ym, xp, xm, xo, zp, zm, co):
        pl.semaphore_signal(
            barrier, inc=1, device_id=peer, device_id_type=pl.DeviceIdType.MESH
        )
    pl.semaphore_wait(barrier, 8)

    def mine(n, h=0):
        return pl.ds(pl.multiple_of(c * 128 + h * 64, 64), n)

    def wcopy(ch, k, src_slots, dst_slots, rows, peer):
        return pltpu.make_async_remote_copy(
            src_ref=wbuf.at[ch, src_slots, rows],
            dst_ref=wbuf.at[ch, dst_slots, rows],
            send_sem=wss.at[ch, k],
            recv_sem=wrs.at[ch, k],
            device_id=peer,
            device_id_type=pl.DeviceIdType.MESH,
        )

    def y_own(ch):
        return [
            wcopy(ch, 0, 0, 1, mine(128), yp),
            wcopy(ch, 1, 0, 2, mine(128), ym),
        ]

    def y_relay(ch):
        return [
            wcopy(ch, 2, 1, 3, mine(64, 0), yp),
            wcopy(ch, 3, 2, 3, mine(64, 1), ym),
        ]

    def x_own(ch):
        return [
            wcopy(ch, 4, 0, 4, mine(64, 0), xp),
            wcopy(ch, 5, 0, 4, mine(64, 1), xm),
        ]

    def x_near(ch):
        near, far = pl.ds(1, 2), pl.ds(5, 2)
        return [
            wcopy(ch, 6, near, far, mine(64, 0), xp),
            wcopy(ch, 7, near, far, mine(64, 1), xm),
        ]

    def x_far(ch):
        return [
            wcopy(ch, 8, 3, 7, mine(64, 0), xp),
            wcopy(ch, 9, 3, 7, mine(64, 1), xm),
        ]

    def c_near(ch):
        return [wcopy(ch, 10, pl.ds(1, 2), pl.ds(1, 2), mine(128), co)]

    def c_far(ch):
        return [wcopy(ch, 11, 3, 3, mine(128), co)]

    def c_side(ch):
        return [wcopy(ch, 12, pl.ds(4, 4), pl.ds(4, 4), mine(128), co)]

    def start(copies):
        for d in copies:
            d.start()

    def arrived(copies):
        for d in copies:
            d.wait_recv()

    def sent(copies):
        for d in copies:
            d.wait_send()

    def step0(ch):
        start(y_own(ch) + x_own(ch))

    def step1(ch):
        arrived(y_own(ch))
        start(y_relay(ch) + x_near(ch) + c_near(ch))

    def step2(ch):
        arrived(y_relay(ch))
        start(x_far(ch) + c_far(ch))

    def step3(ch):
        arrived(x_own(ch) + x_near(ch) + x_far(ch))
        start(c_side(ch))

    def whole(ch):
        arrived(c_near(ch) + c_far(ch) + c_side(ch))

    def kvcopy(k, src, dst, peer):
        g, j, n = dst
        return pltpu.make_async_remote_copy(
            src_ref=kvbuf.at[src[0], 0, pl.ds(src[1], n)],
            dst_ref=kvbuf.at[g, 0, pl.ds(j, n)],
            send_sem=kss.at[g, k],
            recv_sem=krs.at[g, k],
            device_id=peer,
            device_id_type=pl.DeviceIdType.MESH,
        )

    xhi = kvcopy(0, (0, 0), (0, 1, 1), xo)

    def ring(s, j):
        first = isinstance(s, int) and s == 1
        src = (0, j % 2) if first else (s - 1, j)
        return kvcopy(j, src, (s, j, 1), zp if j < 2 else zm)

    last = [
        kvcopy(2, (HALF - 1, 0), (0, 2, 1), zp),
        kvcopy(3, (HALF - 1, 3), (0, 3, 1), zm),
    ]

    def cross(g, j, n, k):
        return pltpu.make_async_remote_copy(
            src_ref=kvbuf.at[g, 0, pl.ds(j, n)],
            dst_ref=kvbuf.at[g, 1, pl.ds(j, n)],
            send_sem=css.at[g, k],
            recv_sem=crs.at[g, k],
            device_id=co,
            device_id_type=pl.DeviceIdType.MESH,
        )

    cross_own = cross(0, 0, 1, 0)
    cross_xhi = cross(0, 1, 1, 1)
    cross_far = cross(0, 2, 2, 2)

    def norm(v, eps=1e-06):
        return lax.rsqrt(jnp.mean(v * v, axis=-1, keepdims=True) + eps)

    def column(slot):
        yy = (y + (0, 3, 1, 2)[slot % 4]) % 4
        xx = xl if slot < 4 else 1 - xl
        return pl.ds(pl.multiple_of((yy * 2 + xx) * HD, HD), HD)

    def projected(ch):
        w = wbuf[ch].reshape(8 * HD, HD)
        return jnp.dot(nrel[...], w, preferred_element_type=F32)

    def rotary(u):
        first, second = u[:, : HD // 2], u[:, HD // 2 :]
        cs, sn = cos[...], sin[...]
        return jnp.concatenate(
            [first * cs - second * sn, second * cs + first * sn], axis=1
        )

    def query(ch, head):
        whole(ch)
        q = rotary(projected(ch)) * HD ** (-0.5)
        qbuf[pl.ds(head * ROWS, ROWS), :] = q.astype(BF16)

    def attend(g):
        kv = kvbuf[g].reshape(8 * ROWS, 2 * HD)
        keys, values = kv[:, :HD], kv[:, HD:]
        s = lax.dot_general(
            qbuf[...], keys, (((1,), (1,)), ((), ())), preferred_element_type=F32
        )
        old = mrow[:, :1]
        new = jnp.maximum(old, jnp.max(s, axis=1, keepdims=True))
        scale = jnp.exp(old - new)
        e = jnp.exp(s - new)
        lrow[...] = lrow[...] * scale + jnp.sum(e, axis=1, keepdims=True)
        mrow[...] = jnp.broadcast_to(new, mrow.shape)
        acc[...] = acc[...] * scale + jnp.dot(
            e.astype(BF16), values, preferred_element_type=F32
        )

    load(0).wait()
    load(1).wait()
    step0(0)
    step0(1)
    for ch in range(2, NCH):
        load(ch).wait()

    hidden = hid[...].astype(F32)
    inv = norm(hidden)
    for slot in range(8):
        col = column(slot)
        part = hid[:, col].astype(F32) * inv * gain[:, col]
        nrel[:, slot * HD : (slot + 1) * HD] = part.astype(BF16)
    acc[...] = jnp.zeros_like(acc)
    lrow[...] = jnp.zeros_like(lrow)
    mrow[...] = jnp.full_like(mrow, -1e30)

    step1(0)
    step1(1)
    step0(2)
    step2(0)
    step2(1)
    step0(3)
    step1(2)
    step3(0)
    step3(1)
    step2(2)
    step1(3)
    step0(4)

    whole(0)
    k = rotary(projected(0))
    kvbuf[0, 0, 0, :, :HD] = k.astype(BF16)
    whole(1)
    kvbuf[0, 0, 0, :, HD:] = projected(1).astype(BF16)

    xhi.start()
    ring(1, 0).start()
    ring(1, 2).start()
    cross_own.start()
    step3(2)
    step2(3)
    step1(4)
    step0(5)
    xhi.wait_recv()
    ring(1, 1).start()
    ring(1, 3).start()
    cross_xhi.start()

    def turn(s):
        for j in range(4):
            ring(s - 1, j).wait_recv()
            ring(s, j).start()
        cross(s - 1, 0, 4, 0).start()

    def weights(i):
        step3(i - 2)
        step2(i - 1)
        step1(i)
        step0(i + 1)

    def early(s, _):
        for j in range(4):
            kvcopy(j, (s - 1, j), (s - 1, j, 1), zp).wait_recv()
            ring(s, j).start()
        cross(s - 1, 0, 4, 0).start()
        weights(s + 3)
        query(s, s - 2)
        return 0

    lax.fori_loop(2, 6, early, 0)

    def groups(a, b):
        def one(g, _):
            cross(g, 0, 4, 0).wait_recv()
            attend(g)
            return 0

        lax.fori_loop(a, b, one, 0)

    turn(6)
    weights(9)
    query(6, 4)
    groups(1, 3)
    turn(7)
    weights(10)
    groups(3, 5)
    for j in range(4):
        ring(HALF - 1, j).wait_recv()
    for d in last:
        d.start()
    cross(HALF - 1, 0, 4, 0).start()
    step3(9)
    step2(10)
    step1(11)
    groups(5, 7)
    for d in last:
        d.wait_recv()
    cross_far.start()
    step3(10)
    step2(11)
    groups(7, 8)
    cross_own.wait_recv()
    cross_xhi.wait_recv()
    cross_far.wait_recv()
    step3(11)
    attend(0)

    att = (acc[...] / lrow[:, :1]).astype(BF16)
    for ch in range(2 + HEADS, NCH):
        whole(ch)
    total = jnp.zeros((ROWS, 1), F32)
    for slot in range(8):
        part = jnp.zeros((ROWS, HD), F32)
        for h in range(HEADS):
            part += jnp.dot(
                att[h * ROWS : (h + 1) * ROWS],
                wbuf[2 + HEADS + h, slot],
                preferred_element_type=F32,
            )
        proj[:, slot * HD : (slot + 1) * HD] = part
        total += jnp.sum(part * part, axis=1, keepdims=True)
    inv2 = lax.rsqrt(total / (8 * HD) + 1e-06)
    for slot in range(8):
        col = column(slot)
        part = proj[:, slot * HD : (slot + 1) * HD] * inv2 * pgain[:, col]
        out[:, col] = (hid[:, col].astype(F32) + part).astype(BF16)

    def drain(ch, _):
        sent(
            y_own(ch) + y_relay(ch) + x_own(ch) + x_near(ch) + x_far(ch)
            + c_near(ch) + c_far(ch) + c_side(ch)
        )
        return 0

    lax.fori_loop(0, NCH, drain, 0)

    def drain_ring(g, _):
        for j in range(4):
            kvcopy(j, (g, j), (g, j, 1), zp).wait_send()
        cross(g, 0, 4, 0).wait_send()
        return 0

    lax.fori_loop(1, HALF, drain_ring, 0)
    sent([xhi, cross_own, cross_xhi, cross_far] + last)


def local(hidden_in, attn_gain, w_query, w_keyval, w_output, post_gain):
    count, width = hidden_in.shape[1:]
    freq = jnp.exp(-jnp.log(10000.0) * jnp.arange(HD // 2, dtype=F32) * 2.0 / HD)
    positions = lax.axis_index("seq") * count + jnp.arange(count, dtype=jnp.int32)
    angle = positions.astype(F32)[:, None] * freq[None, :]
    vmem = pl.BlockSpec(memory_space=pltpu.VMEM)
    hbm = pl.BlockSpec(memory_space=pl.ANY)
    dma = pltpu.SemaphoreType.DMA
    result = pl.pallas_call(
        ring_kernel,
        out_shape=jax.ShapeDtypeStruct((count, width), BF16),
        in_specs=[vmem] * 5 + [hbm] * 3,
        out_specs=vmem,
        scratch_shapes=[
            pltpu.VMEM((NCH, 8, HD, HD), BF16),
            pltpu.VMEM((HALF, 2, 4, ROWS, 2 * HD), BF16),
            pltpu.VMEM((ROWS, 8 * HD), BF16),
            pltpu.VMEM((HEADS * ROWS, HD), BF16),
            pltpu.VMEM((HEADS * ROWS, HD), F32),
            pltpu.VMEM((HEADS * ROWS, 128), F32),
            pltpu.VMEM((HEADS * ROWS, 128), F32),
            pltpu.VMEM((ROWS, 8 * HD), F32),
            dma((NCH,)),
            dma((NCH, 13)),
            dma((NCH, 13)),
            dma((HALF, 4)),
            dma((HALF, 4)),
            dma((HALF, 3)),
            dma((HALF, 3)),
        ],
        compiler_params=pltpu.CompilerParams(
            collective_id=0, has_side_effects=True, vmem_limit_bytes=60 * 1024 * 1024
        ),
    )(
        hidden_in[0], attn_gain[None], jnp.cos(angle), jnp.sin(angle), post_gain[None],
        w_query, w_keyval, w_output,
    )
    return result[None]


def solution(mesh):
    return jax.shard_map(
        local,
        mesh=mesh,
        in_specs=(
            P("dp", "seq", None), P(), P("dp", None), P("dp", None), P(None, "dp"), P(),
        ),
        out_specs=P("dp", "seq", None),
        check_vma=False,
    )
```

time: 234 us -> 82.7 us (0.35)
  the two profiles are of different devices: /device:TPU:32 before, /device:TPU:1 now
where the time goes in v1:
time: 82.7 us; the launch traced here: 82.5 us
  Pallas kernels  80 us (97%)
  local copies, waits for them, and re-layouts  1.67 us (2%)
  other arithmetic  0.84 us (1%)
    pallas_call x1, Pallas kernels, local(): pl.pallas_call(ring_kernel, out_shape=jax.ShapeDtypeStruct((count, width)...  80 us
    unnamed x1, local copies, waits for them, and re-layouts  1.67 us

profile of v1, /device:TPU:1, one launch (start us, length us, event | category | flops | bytes accessed | tf_op | source)
XLA Modules:
  0.0 82.5 jit_solution(15775644693519445138)
XLA Ops:
  0.0 0.8 multiply_sine_fusion
  0.8 80.0 %shard_map.64 = bf16[64,2048]{1,0:T(8,128)(2,1)} custom-call(bf16[64,2048]{1,0:T(8,128)(2,1)} %bitcast.5, f32[1,2048]{1,0:T(1,128)} %bitcast.6, f32[64,128]{1,0:T(8,128)} %get-tuple-element.6.cos, f32[64,128]{1,0:T(8,128)} %get-tuple-element.5.sin, f32[1,2048]{1,0:T(1,128)} %bitcast.7, bf16[256,1280]{1,0:T(8,128)(2,1)} %wq.1, bf16[256,512]{1,0:T(8,128)(2,1)} %wkv.1, ...), custom_call_target="tpu_custom_call" | custom-call | tf_op jit(solution)/shard_map/pallas_call | solution.py:377
  80.8 1.7 %copy.8 = bf16[1,64,2048]{2,1,0:T(8,128)(2,1)} copy(bf16[1,64,2048]{2,1,0:T(8,128)(2,1)} %bitcast.4) | data formatting | bytes 524288
  (2 shorter events, 0.0 us)

commit v2 on v0

v2 whole, which is shorter than its diff:
```python
import jax
import jax.numpy as jnp
import numpy as np
from jax import lax
from jax.experimental import pallas as pl
from jax.experimental.pallas import tpu as pltpu
from jax.sharding import PartitionSpec as P

BF16 = jnp.bfloat16
F32 = jnp.float32

ROWS = 64
HD = 256
HEADS = 5
QS, OS = 2, 2 + HEADS
NCH = OS + HEADS
NZ = 16
HALF = NZ // 2
MESH = pl.DeviceIdType.MESH


def ring_kernel(
    hid, gain, crow, srow, cbase, sbase, pgain, wq, wkv, wo, out,
    wbuf, kvbuf, nrel, qbuf, qout, acc, mrow, lrow, proj, cos, sin,
    lsem, wss, wcs, wrs, wrc, krs, kss, xss, xrs, css, crs, nss, nrs, qss, qrs,
):
    dp = lax.axis_index("dp")
    sq = lax.axis_index("seq")
    y, xl = dp // 2, dp % 2
    xh, z, c = sq // 32, (sq // 2) % NZ, sq % 2

    def dev(yy, xll, xhh, zz, cc):
        return (yy * 2 + xll, xhh * 32 + zz * 2 + cc)

    yp = dev((y + 1) % 4, xl, xh, z, c)
    ym = dev((y + 3) % 4, xl, xh, z, c)
    xp = dev(y, 1 - xl, (xh + xl) % 2, z, c)
    xm = dev(y, 1 - xl, (xh + 1 - xl) % 2, z, c)
    xo = dev(y, xl, 1 - xh, z, c)
    zp = dev(y, xl, xh, (z + 1) % NZ, c)
    zm = dev(y, xl, xh, (z + NZ - 1) % NZ, c)
    co = dev(y, xl, xh, z, 1 - c)

    def remote(src, dst, ssem, rsem, peer):
        return pltpu.make_async_remote_copy(
            src_ref=src, dst_ref=dst, send_sem=ssem, recv_sem=rsem,
            device_id=peer, device_id_type=MESH,
        )

    def awaited(ref, sem):
        pltpu.make_async_copy(ref, ref, sem).wait()

    def load(ch):
        if ch < QS:
            src = wkv.at[:, pl.ds(ch * HD, HD)]
        elif ch < OS:
            src = wq.at[:, pl.ds((ch - QS) * HD, HD)]
        else:
            src = wo.at[pl.ds((ch - OS) * HD, HD), :]
        sem = lsem.at[0 if ch < QS else 1]
        pltpu.make_async_copy(src, wbuf.at[ch, 0], sem).start()

    @pl.when(c == 1)
    def _():
        for ch in (0, 1, *range(OS, NCH)):
            load(ch)

    @pl.when(c == 0)
    def _():
        for ch in range(QS, NCH):
            load(ch)

    barrier = pltpu.get_barrier_semaphore()
    for peer in (yp, ym, xp, xm, xo, zp, zm, co):
        pl.semaphore_signal(barrier, inc=1, device_id=peer, device_id_type=MESH)
    pl.semaphore_wait(barrier, 8)

    top, bottom, every = pl.ds(0, 128), pl.ds(128, 128), pl.ds(0, 256)

    def wcopy(ch, kind, src, dst, rows, peer):
        remote(
            wbuf.at[ch, src, rows], wbuf.at[ch, dst, rows],
            wss.at[0], wrs.at[ch, kind], peer,
        ).start()

    def step0(ch):
        wcopy(ch, 0, 0, 1, every, yp)
        wcopy(ch, 0, 0, 2, every, ym)
        wcopy(ch, 2, 0, 4, top, xp)
        wcopy(ch, 2, 0, 4, bottom, xm)

    def step1(ch):
        awaited(wbuf.at[ch, pl.ds(1, 2)], wrs.at[ch, 0])
        wcopy(ch, 1, 1, 3, top, yp)
        wcopy(ch, 1, 2, 3, bottom, ym)
        wcopy(ch, 2, pl.ds(1, 2), pl.ds(5, 2), top, xp)
        wcopy(ch, 2, pl.ds(1, 2), pl.ds(5, 2), bottom, xm)

    def step2(ch):
        awaited(wbuf.at[ch, 3], wrs.at[ch, 1])
        wcopy(ch, 2, 3, 7, top, xp)
        wcopy(ch, 2, 3, 7, bottom, xm)

    def step3(ch):
        awaited(wbuf.at[ch, pl.ds(4, 4)], wrs.at[ch, 2])

    def pass_on(ch, slots):
        ref = wbuf.at[ch, slots]
        remote(ref, ref, wcs.at[0], wrc.at[ch - OS], co).start()

    def give(ch):
        pass_on(ch, pl.ds(1, 3))
        step3(ch)
        pass_on(ch, pl.ds(4, 4))

    def hop(src, dst, half, peer):
        remote(
            kvbuf.at[src[0], src[1], half], kvbuf.at[dst[0], dst[1], half],
            kss.at[0], krs.at[dst[0], dst[1] // 2, half], peer,
        ).start()

    def hops(s, ab, half, first=False):
        for way, peer in ((0, zp), (1, zm)):
            src = (0, 2 * ab) if first else (s - 1, 2 * ab + way)
            hop(src, (s, 2 * ab + way), half, peer)

    def landed(s, ab, half):
        awaited(kvbuf.at[s, pl.ds(2 * ab, 2), half], krs.at[s, ab, half])

    def cross(g, js, k):
        ref = kvbuf.at[g, js]
        return remote(ref, ref, css.at[0], crs.at[g, k], co)

    def column(slot):
        yy = (y + (0, 3, 1, 2)[slot % 4]) % 4
        xx = xl if slot < 4 else 1 - xl
        return pl.ds(pl.multiple_of((yy * 2 + xx) * HD, HD), HD)

    def normalize():
        hidden = hid[...].astype(F32)
        inv = lax.rsqrt(jnp.mean(hidden * hidden, axis=-1, keepdims=True) + 1e-06)
        own = pl.ds(pl.multiple_of(c * ROWS, ROWS), ROWS)
        for slot in range(8):
            col = column(slot)
            part = hid[:, col].astype(F32) * inv * gain[:, col]
            nrel[own, slot * HD : (slot + 1) * HD] = part.astype(BF16)
        remote(nrel.at[own], nrel.at[own], nss.at[0], nrs.at[0], co).start()
        at = pl.ds(sq // 2, 1)
        cb, sb = cbase[at, :], sbase[at, :]
        cr, sr = crow[...], srow[...]
        cos[...] = cb * cr - sb * sr
        sin[...] = sb * cr + cb * sr
        acc[...] = jnp.zeros_like(acc)
        lrow[...] = jnp.zeros_like(lrow)
        mrow[...] = jnp.full_like(mrow, -1e30)

    def partner_rows():
        other = pl.ds(pl.multiple_of((1 - c) * ROWS, ROWS), ROWS)
        awaited(nrel.at[other], nrs.at[0])

    def projected(ch):
        w = wbuf[ch].reshape(8 * HD, HD)
        return jnp.dot(nrel[...], w, preferred_element_type=F32)

    def rotary(u):
        first, second = u[:, : HD // 2], u[:, HD // 2 :]
        cs, sn = cos[...], sin[...]
        return jnp.concatenate(
            [first * cs - second * sn, second * cs + first * sn], axis=1
        )

    def query(h):
        q = (rotary(projected(QS + h)) * HD ** (-0.5)).astype(BF16)
        qbuf[h] = q[:ROWS]
        qout[h] = q[ROWS:]
        remote(qout.at[h], qbuf.at[h], qss.at[0], qrs.at[0], co).start()

    def attend(g):
        kv = kvbuf[g].reshape(8 * ROWS, 2 * HD)
        keys, values = kv[:, :HD], kv[:, HD:]
        q = qbuf[...].reshape(HEADS * ROWS, HD)
        s = lax.dot_general(
            q, keys, (((1,), (1,)), ((), ())), preferred_element_type=F32
        )
        old = mrow[:, :1]
        new = jnp.maximum(old, jnp.max(s, axis=1, keepdims=True))
        scale = jnp.exp(old - new)
        e = jnp.exp(s - new)
        lrow[...] = lrow[...] * scale + jnp.sum(e, axis=1, keepdims=True)
        mrow[...] = jnp.broadcast_to(new, mrow.shape)
        acc[...] = acc[...] * scale + jnp.dot(
            e.astype(BF16), values, preferred_element_type=F32
        )

    def finish():
        att = (acc[...] / lrow[:, :1]).astype(BF16)
        total = jnp.zeros((ROWS, 1), F32)
        for slot in range(8):
            part = jnp.zeros((ROWS, HD), F32)
            for h in range(HEADS):
                part += jnp.dot(
                    att[h * ROWS : (h + 1) * ROWS], wbuf[OS + h, slot],
                    preferred_element_type=F32,
                )
            proj[:, slot * HD : (slot + 1) * HD] = part
            total += jnp.sum(part * part, axis=1, keepdims=True)
        inv = lax.rsqrt(total / (8 * HD) + 1e-06)
        for slot in range(8):
            col = column(slot)
            part = proj[:, slot * HD : (slot + 1) * HD] * inv * pgain[:, col]
            out[:, col] = (hid[:, col].astype(F32) + part).astype(BF16)

    @pl.when(c == 1)
    def _():
        awaited(wbuf.at[pl.ds(0, 2), 0], lsem.at[0])
        step0(0)
        step0(1)
        normalize()
        step1(0)
        step1(1)
        step2(0)
        step2(1)
        partner_rows()
        step3(0)
        k = rotary(projected(0)).astype(BF16)
        kvbuf[0, 0, :, :, :HD] = k.reshape(2, ROWS, HD)
        step3(1)
        v = projected(1).astype(BF16)
        kvbuf[0, 0, :, :, HD:] = v.reshape(2, ROWS, HD)
        for half in range(2):
            remote(
                kvbuf.at[0, 0, half], kvbuf.at[0, 2, half],
                xss.at[0], xrs.at[half], xo,
            ).start()
            hops(1, 0, half, True)
        cross(0, 0, 0).start()
        for half in range(2):
            awaited(kvbuf.at[0, 2, half], xrs.at[half])
            hops(1, 1, half, True)
        cross(0, 2, 1).start()

        def turn(s, ab):
            for half in range(2):
                landed(s - 1, ab, half)
                hops(s, ab, half)

        def early(s, _):
            turn(s, 0)
            turn(s, 1)
            cross(s - 1, pl.ds(0, 4), 0).start()
            return 0

        lax.fori_loop(2, 6, early, 0)

        turn(6, 0)
        turn(6, 1)
        cross(5, pl.ds(0, 4), 0).start()
        awaited(qbuf, qrs.at[0])
        attend(1)
        turn(7, 0)
        attend(2)
        turn(7, 1)
        cross(6, pl.ds(0, 4), 0).start()
        attend(3)
        for half in range(2):
            landed(HALF - 1, 0, half)
            hop((HALF - 1, 0), (0, 1), half, zp)
        attend(4)
        for half in range(2):
            landed(HALF - 1, 1, half)
            hop((HALF - 1, 3), (0, 3), half, zm)
        cross(HALF - 1, pl.ds(0, 4), 0).start()

        def rest(g, _):
            attend(g)
            return 0

        lax.fori_loop(5, HALF, rest, 0)
        for ab in range(2):
            for half in range(2):
                awaited(kvbuf.at[0, 2 * ab + 1, half], krs.at[0, ab, half])
            cross(0, 2 * ab + 1, 2 + ab).start()
        attend(0)
        awaited(wbuf.at[pl.ds(OS, HEADS), 0], lsem.at[1])
        for ch in range(OS, NCH):
            awaited(wbuf.at[ch, pl.ds(1, 7)], wrc.at[ch - OS])
        finish()
        awaited(wbuf.at[pl.ds(0, 2), pl.ds(0, 7)], wss.at[0])
        awaited(wbuf.at[pl.ds(0, 6), pl.ds(0, 5)], kss.at[0])
        awaited(kvbuf.at[0, 0], xss.at[0])
        awaited(kvbuf, css.at[0])

    @pl.when(c == 0)
    def _():
        normalize()
        awaited(wbuf.at[pl.ds(QS, 2 * HEADS), 0], lsem.at[1])
        step0(2)
        partner_rows()
        step0(3)
        step1(2)
        step0(4)
        step1(3)
        step2(2)
        step0(5)

        def queries(i, _):
            step1(i)
            step2(i - 1)
            step0(i + 2)
            step3(i - 2)
            query(i - QS - 2)
            return 0

        lax.fori_loop(4, 9, queries, 0)

        def near(g):
            awaited(kvbuf.at[g], crs.at[g, 0])
            attend(g)

        step1(9)
        step2(8)
        step0(11)
        give(7)
        near(1)
        step1(10)
        step2(9)
        near(2)
        give(8)
        step1(11)
        step2(10)
        near(3)
        give(9)
        step2(11)
        near(4)
        give(10)
        near(5)
        give(11)
        near(6)
        near(7)
        for j, k in ((0, 0), (2, 1), (1, 2), (3, 3)):
            awaited(kvbuf.at[0, j], crs.at[0, k])
        attend(0)
        finish()
        awaited(wbuf.at[pl.ds(QS, 2 * HEADS), pl.ds(0, 7)], wss.at[0])
        awaited(wbuf.at[pl.ds(OS, HEADS), pl.ds(1, 7)], wcs.at[0])
        awaited(qout, qss.at[0])

    own = pl.ds(pl.multiple_of(c * ROWS, ROWS), ROWS)
    awaited(nrel.at[own], nss.at[0])


def local(hidden_in, attn_gain, w_query, w_keyval, w_output, post_gain):
    count, width = hidden_in.shape[1:]
    freq = 10000.0 ** (-np.arange(HD // 2) * 2.0 / HD)
    row = np.arange(2 * ROWS)[:, None] * freq
    base = np.arange(2 * NZ)[:, None] * (2 * ROWS) * freq
    tables = [np.asarray(f(a), np.float32) for a in (row, base) for f in (np.cos, np.sin)]
    vmem = pl.BlockSpec(memory_space=pltpu.VMEM)
    hbm = pl.BlockSpec(memory_space=pltpu.HBM)
    dma = pltpu.SemaphoreType.DMA
    result = pl.pallas_call(
        ring_kernel,
        out_shape=jax.ShapeDtypeStruct((count, width), BF16),
        in_specs=[vmem] * 7 + [hbm] * 3,
        out_specs=vmem,
        scratch_shapes=[
            pltpu.VMEM((NCH, 8, HD, HD), BF16),
            pltpu.VMEM((HALF, 4, 2, ROWS, 2 * HD), BF16),
            pltpu.VMEM((2 * ROWS, 8 * HD), BF16),
            pltpu.VMEM((HEADS, ROWS, HD), BF16),
            pltpu.VMEM((HEADS, ROWS, HD), BF16),
            pltpu.VMEM((HEADS * ROWS, HD), F32),
            pltpu.VMEM((HEADS * ROWS, 128), F32),
            pltpu.VMEM((HEADS * ROWS, 128), F32),
            pltpu.VMEM((ROWS, 8 * HD), F32),
            pltpu.VMEM((2 * ROWS, HD // 2), F32),
            pltpu.VMEM((2 * ROWS, HD // 2), F32),
            dma((2,)),
            dma((1,)),
            dma((1,)),
            dma((NCH, 3)),
            dma((HEADS,)),
            dma((HALF, 2, 2)),
            dma((1,)),
            dma((1,)),
            dma((2,)),
            dma((1,)),
            dma((HALF, 4)),
            dma((1,)),
            dma((1,)),
            dma((1,)),
            dma((1,)),
        ],
        compiler_params=pltpu.CompilerParams(
            collective_id=0, has_side_effects=True, vmem_limit_bytes=60 * 1024 * 1024
        ),
    )(
        hidden_in[0], attn_gain[None], *tables, post_gain[None],
        w_query, w_keyval, w_output,
    )
    return result[None]


def solution(mesh):
    return jax.shard_map(
        local,
        mesh=mesh,
        in_specs=(
            P("dp", "seq", None), P(), P("dp", None), P("dp", None), P(None, "dp"), P(),
        ),
        out_specs=P("dp", "seq", None),
        check_vma=False,
    )
```

time: 234 us -> 64.7 us (0.28)
  the two profiles are of different devices: /device:TPU:32 before, /device:TPU:1 now
where the time goes in v2:
time: 64.7 us; the launch traced here: 64.6 us
  Pallas kernels  62.9 us (97%)
  local copies, waits for them, and re-layouts  1.67 us (3%)
    pallas_call x1, Pallas kernels, local(): pl.pallas_call(ring_kernel, out_shape=jax.ShapeDtypeStruct((count, width)...  62.9 us
    unnamed x1, local copies, waits for them, and re-layouts  1.67 us

profile of v2, /device:TPU:1, one launch (start us, length us, event | category | flops | bytes accessed | tf_op | source)
XLA Modules:
  0.0 64.6 jit_solution(4781697545413217097)
XLA Ops:
  0.0 62.9 %shard_map.100 = bf16[64,2048]{1,0:T(8,128)(2,1)} custom-call(bf16[64,2048]{1,0:T(8,128)(2,1)} %bitcast.5, f32[1,2048]{1,0:T(1,128)} %bitcast.6, f32[128,128]{1,0:T(8,128)} %constant.8.clone.crow, f32[128,128]{1,0:T(8,128)} %constant.9.clone.srow, f32[32,128]{1,0:T(8,128)} %constant.10.clone.cbase, f32[32,128]{1,0:T(8,128)} %constant.11.clone.sbase, ...), custom_call_target="tpu_custom_call" | custom-call | tf_op jit(solution)/shard_map/pallas_call | solution.py:361
  62.9 1.7 %copy.12 = bf16[1,64,2048]{2,1,0:T(8,128)(2,1)} copy(bf16[1,64,2048]{2,1,0:T(8,128)(2,1)} %bitcast.4) | data formatting | bytes 524288

commit v3 on v2

--- a/solution.py
+++ b/solution.py
@@ -16,12 +16,14 @@
 NCH = OS + HEADS
 NZ = 16
 HALF = NZ // 2
+PIECES = 4
+PIECE = 2 * ROWS // PIECES
 MESH = pl.DeviceIdType.MESH
 
 
 def ring_kernel(
-    hid, gain, crow, srow, cbase, sbase, pgain, wq, wkv, wo, out,
-    wbuf, kvbuf, nrel, qbuf, qout, acc, mrow, lrow, proj, cos, sin,
+    hid_in, gain_in, crow_in, srow_in, cbase_in, sbase_in, pgain_in, wq, wkv, wo, out,
+    hid, gain, crow, srow, cbase, sbase, pgain, wbuf, kvbuf, nrel, qbuf, qout, acc, mrow, lrow, proj, cos, sin,
     lsem, wss, wcs, wrs, wrc, krs, kss, xss, xrs, css, crs, nss, nrs, qss, qrs,
 ):
     dp = lax.axis_index("dp")
@@ -49,6 +51,10 @@
 
     def awaited(ref, sem):
         pltpu.make_async_copy(ref, ref, sem).wait()
+
+    barrier = pltpu.get_barrier_semaphore()
+    for peer in (yp, ym, xp, xm, xo, zp, zm, co):
+        pl.semaphore_signal(barrier, inc=1, device_id=peer, device_id_type=MESH)
 
     def load(ch):
         if ch < QS:
@@ -60,9 +66,27 @@
         sem = lsem.at[0 if ch < QS else 1]
         pltpu.make_async_copy(src, wbuf.at[ch, 0], sem).start()
 
+    small = [
+        pltpu.make_async_copy(src, dst, lsem.at[2 + i])
+        for i, (src, dst) in enumerate(
+            [
+                (hid_in, hid), (gain_in, gain), (crow_in, crow), (srow_in, srow),
+                (cbase_in, cbase), (sbase_in, sbase), (pgain_in, pgain),
+            ]
+        )
+    ]
+
     @pl.when(c == 1)
     def _():
-        for ch in (0, 1, *range(OS, NCH)):
+        for ch in (0, 1):
+            load(ch)
+
+    for copy in small:
+        copy.start()
+
+    @pl.when(c == 1)
+    def _():
+        for ch in range(OS, NCH):
             load(ch)
 
     @pl.when(c == 0)
@@ -70,9 +94,6 @@
         for ch in range(QS, NCH):
             load(ch)
 
-    barrier = pltpu.get_barrier_semaphore()
-    for peer in (yp, ym, xp, xm, xo, zp, zm, co):
-        pl.semaphore_signal(barrier, inc=1, device_id=peer, device_id_type=MESH)
     pl.semaphore_wait(barrier, 8)
 
     top, bottom, every = pl.ds(0, 128), pl.ds(128, 128), pl.ds(0, 256)
@@ -104,6 +125,23 @@
     def step3(ch):
         awaited(wbuf.at[ch, pl.ds(4, 4)], wrs.at[ch, 2])
 
+    def xstep1(ch):
+        awaited(wbuf.at[ch, pl.ds(1, 2)], wrs.at[ch, 0])
+        wcopy(ch, 1, 1, 3, top, yp)
+        wcopy(ch, 1, 2, 3, bottom, ym)
+        awaited(wbuf.at[ch, 4], wrs.at[ch, 2])
+        wcopy(ch, 3, 4, 5, every, yp)
+        wcopy(ch, 3, 4, 6, every, ym)
+
+    def xstep2(ch):
+        awaited(wbuf.at[ch, pl.ds(5, 2)], wrs.at[ch, 3])
+        wcopy(ch, 4, 5, 7, top, yp)
+        wcopy(ch, 4, 6, 7, bottom, ym)
+
+    def xstep3(ch):
+        awaited(wbuf.at[ch, 3], wrs.at[ch, 1])
+        awaited(wbuf.at[ch, 7], wrs.at[ch, 4])
+
     def pass_on(ch, slots):
         ref = wbuf.at[ch, slots]
         remote(ref, ref, wcs.at[0], wrc.at[ch - OS], co).start()
@@ -137,6 +175,8 @@
         return pl.ds(pl.multiple_of((yy * 2 + xx) * HD, HD), HD)
 
     def normalize():
+        for copy in small:
+            copy.wait()
         hidden = hid[...].astype(F32)
         inv = lax.rsqrt(jnp.mean(hidden * hidden, axis=-1, keepdims=True) + 1e-06)
         own = pl.ds(pl.multiple_of(c * ROWS, ROWS), ROWS)
@@ -144,7 +184,6 @@
             col = column(slot)
             part = hid[:, col].astype(F32) * inv * gain[:, col]
             nrel[own, slot * HD : (slot + 1) * HD] = part.astype(BF16)
-        remote(nrel.at[own], nrel.at[own], nss.at[0], nrs.at[0], co).start()
         at = pl.ds(sq // 2, 1)
         cb, sb = cbase[at, :], sbase[at, :]
         cr, sr = crow[...], srow[...]
@@ -154,6 +193,10 @@
         lrow[...] = jnp.zeros_like(lrow)
         mrow[...] = jnp.full_like(mrow, -1e30)
 
+    def give_rows():
+        own = pl.ds(pl.multiple_of(c * ROWS, ROWS), ROWS)
+        remote(nrel.at[own], nrel.at[own], nss.at[0], nrs.at[0], co).start()
+
     def partner_rows():
         other = pl.ds(pl.multiple_of((1 - c) * ROWS, ROWS), ROWS)
         awaited(nrel.at[other], nrs.at[0])
@@ -176,7 +219,16 @@
         remote(qout.at[h], qbuf.at[h], qss.at[0], qrs.at[0], co).start()
 
     def attend(g):
-        kv = kvbuf[g].reshape(8 * ROWS, 2 * HD)
+        online(kvbuf[g].reshape(8 * ROWS, 2 * HD))
+
+    def attend_way(way):
+        online(
+            jnp.concatenate(
+                [kvbuf[0, 2 * ab + way].reshape(2 * ROWS, 2 * HD) for ab in range(2)]
+            )
+        )
+
+    def online(kv):
         keys, values = kv[:, :HD], kv[:, HD:]
         q = qbuf[...].reshape(HEADS * ROWS, HD)
         s = lax.dot_general(
@@ -217,70 +269,82 @@
         step0(1)
         normalize()
         step1(0)
+        give_rows()
         step1(1)
         step2(0)
         step2(1)
         partner_rows()
         step3(0)
         k = rotary(projected(0)).astype(BF16)
-        kvbuf[0, 0, :, :, :HD] = k.reshape(2, ROWS, HD)
+        kvbuf[0, 0, :, :, :HD] = k.reshape(PIECES, PIECE, HD)
+
+        def first(cols):
+            for half in range(PIECES):
+                remote(
+                    kvbuf.at[0, 0, half, :, cols], kvbuf.at[0, 2, half, :, cols],
+                    xss.at[0], xrs.at[half], xo,
+                ).start()
+                for way, peer in ((0, zp), (1, zm)):
+                    remote(
+                        kvbuf.at[0, 0, half, :, cols], kvbuf.at[1, way, half, :, cols],
+                        kss.at[0], krs.at[1, 0, half], peer,
+                    ).start()
+
+        first(pl.ds(0, HD))
         step3(1)
         v = projected(1).astype(BF16)
-        kvbuf[0, 0, :, :, HD:] = v.reshape(2, ROWS, HD)
-        for half in range(2):
-            remote(
-                kvbuf.at[0, 0, half], kvbuf.at[0, 2, half],
-                xss.at[0], xrs.at[half], xo,
-            ).start()
-            hops(1, 0, half, True)
+        kvbuf[0, 0, :, :, HD:] = v.reshape(PIECES, PIECE, HD)
+        first(pl.ds(HD, HD))
         cross(0, 0, 0).start()
-        for half in range(2):
+
+        def turn(s, ab):
+            for half in range(PIECES):
+                landed(s - 1, ab, half)
+                hops(s, ab, half)
+
+        turn(2, 0)
+        for half in range(PIECES):
             awaited(kvbuf.at[0, 2, half], xrs.at[half])
             hops(1, 1, half, True)
         cross(0, 2, 1).start()
 
-        def turn(s, ab):
-            for half in range(2):
-                landed(s - 1, ab, half)
-                hops(s, ab, half)
-
         def early(s, _):
             turn(s, 0)
-            turn(s, 1)
-            cross(s - 1, pl.ds(0, 4), 0).start()
+            turn(s - 1, 1)
+            cross(s - 2, pl.ds(0, 4), 0).start()
             return 0
 
-        lax.fori_loop(2, 6, early, 0)
+        lax.fori_loop(3, 6, early, 0)
 
         turn(6, 0)
-        turn(6, 1)
-        cross(5, pl.ds(0, 4), 0).start()
+        turn(5, 1)
+        cross(4, pl.ds(0, 4), 0).start()
         awaited(qbuf, qrs.at[0])
+        attend_way(0)
         attend(1)
         turn(7, 0)
         attend(2)
-        turn(7, 1)
-        cross(6, pl.ds(0, 4), 0).start()
+        turn(6, 1)
+        cross(5, pl.ds(0, 4), 0).start()
         attend(3)
-        for half in range(2):
+        for half in range(PIECES):
             landed(HALF - 1, 0, half)
             hop((HALF - 1, 0), (0, 1), half, zp)
         attend(4)
-        for half in range(2):
+        turn(7, 1)
+        cross(6, pl.ds(0, 4), 0).start()
+        attend(5)
+        for half in range(PIECES):
             landed(HALF - 1, 1, half)
             hop((HALF - 1, 3), (0, 3), half, zm)
         cross(HALF - 1, pl.ds(0, 4), 0).start()
-
-        def rest(g, _):
-            attend(g)
-            return 0
-
-        lax.fori_loop(5, HALF, rest, 0)
+        attend(6)
+        attend(7)
         for ab in range(2):
-            for half in range(2):
+            for half in range(PIECES):
                 awaited(kvbuf.at[0, 2 * ab + 1, half], krs.at[0, ab, half])
             cross(0, 2 * ab + 1, 2 + ab).start()
-        attend(0)
+        attend_way(1)
         awaited(wbuf.at[pl.ds(OS, HEADS), 0], lsem.at[1])
         for ch in range(OS, NCH):
             awaited(wbuf.at[ch, pl.ds(1, 7)], wrc.at[ch - OS])
@@ -292,54 +356,76 @@
 
     @pl.when(c == 0)
     def _():
-        normalize()
         awaited(wbuf.at[pl.ds(QS, 2 * HEADS), 0], lsem.at[1])
         step0(2)
+        normalize()
+        give_rows()
         partner_rows()
-        step0(3)
-        step1(2)
-        step0(4)
-        step1(3)
-        step2(2)
-        step0(5)
-
-        def queries(i, _):
-            step1(i)
-            step2(i - 1)
-            step0(i + 2)
-            step3(i - 2)
-            query(i - QS - 2)
-            return 0
-
-        lax.fori_loop(4, 9, queries, 0)
 
         def near(g):
             awaited(kvbuf.at[g], crs.at[g, 0])
             attend(g)
 
+        def near_own():
+            for j, k in ((0, 0), (2, 1)):
+                awaited(kvbuf.at[0, j], crs.at[0, k])
+            attend_way(0)
+
+        step0(3)
+        step0(4)
+        step1(2)
+        step0(5)
+        step1(3)
+        step0(6)
+        xstep1(4)
+        step2(2)
+        step0(7)
+        step1(5)
+        step2(3)
+        step0(8)
+        step1(6)
+        xstep2(4)
+        step0(9)
+        step3(2)
+        query(0)
+        step1(7)
+        step2(5)
+        step0(10)
+        step3(3)
+        query(1)
+        step1(8)
+        step2(6)
+        step0(11)
+        xstep3(4)
+        query(2)
         step1(9)
+        step2(7)
+        step3(5)
+        query(3)
+        step1(10)
         step2(8)
-        step0(11)
+        step3(6)
+        query(4)
+        step1(11)
+        step2(9)
+        near_own()
         give(7)
+        step2(10)
         near(1)
-        step1(10)
-        step2(9)
+        give(8)
+        step2(11)
         near(2)
-        give(8)
-        step1(11)
-        step2(10)
+        give(9)
         near(3)
-        give(9)
-        step2(11)
         near(4)
         give(10)
         near(5)
+        near(6)
         give(11)
-        near(6)
         near(7)
-        for j, k in ((0, 0), (2, 1), (1, 2), (3, 3)):
+        for j, k in ((1, 2), (3, 3)):
             awaited(kvbuf.at[0, j], crs.at[0, k])
-        attend(0)
+        attend_way(1)
         finish()
         awaited(wbuf.at[pl.ds(QS, 2 * HEADS), pl.ds(0, 7)], wss.at[0])
         awaited(wbuf.at[pl.ds(OS, HEADS), pl.ds(1, 7)], wcs.at[0])
@@ -356,16 +442,27 @@
     base = np.arange(2 * NZ)[:, None] * (2 * ROWS) * freq
     tables = [np.asarray(f(a), np.float32) for a in (row, base) for f in (np.cos, np.sin)]
     vmem = pl.BlockSpec(memory_space=pltpu.VMEM)
-    hbm = pl.BlockSpec(memory_space=pltpu.HBM)
+    hbm = pl.BlockSpec(memory_space=pl.ANY)
     dma = pltpu.SemaphoreType.DMA
+    operands = [
+        hidden_in[0], attn_gain[None], *tables, post_gain[None],
+        w_query, w_keyval, w_output,
+    ]
     result = pl.pallas_call(
         ring_kernel,
         out_shape=jax.ShapeDtypeStruct((count, width), BF16),
-        in_specs=[vmem] * 7 + [hbm] * 3,
+        in_specs=[hbm] * 10,
         out_specs=vmem,
         scratch_shapes=[
+            pltpu.VMEM((count, width), BF16),
+            pltpu.VMEM((1, width), F32),
+            pltpu.VMEM((2 * ROWS, HD // 2), F32),
+            pltpu.VMEM((2 * ROWS, HD // 2), F32),
+            pltpu.VMEM((2 * NZ, HD // 2), F32),
+            pltpu.VMEM((2 * NZ, HD // 2), F32),
+            pltpu.VMEM((1, width), F32),
             pltpu.VMEM((NCH, 8, HD, HD), BF16),
-            pltpu.VMEM((HALF, 4, 2, ROWS, 2 * HD), BF16),
+            pltpu.VMEM((HALF, 4, PIECES, PIECE, 2 * HD), BF16),
             pltpu.VMEM((2 * ROWS, 8 * HD), BF16),
             pltpu.VMEM((HEADS, ROWS, HD), BF16),
             pltpu.VMEM((HEADS, ROWS, HD), BF16),
@@ -375,15 +472,15 @@
             pltpu.VMEM((ROWS, 8 * HD), F32),
             pltpu.VMEM((2 * ROWS, HD // 2), F32),
             pltpu.VMEM((2 * ROWS, HD // 2), F32),
-            dma((2,)),
-            dma((1,)),
-            dma((1,)),
-            dma((NCH, 3)),
+            dma((9,)),
+            dma((1,)),
+            dma((1,)),
+            dma((NCH, 5)),
             dma((HEADS,)),
-            dma((HALF, 2, 2)),
-            dma((1,)),
-            dma((1,)),
-            dma((2,)),
+            dma((HALF, 2, PIECES)),
+            dma((1,)),
+            dma((1,)),
+            dma((PIECES,)),
             dma((1,)),
             dma((HALF, 4)),
             dma((1,)),
@@ -392,11 +489,10 @@
             dma((1,)),
         ],
         compiler_params=pltpu.CompilerParams(
-            collective_id=0, has_side_effects=True, vmem_limit_bytes=60 * 1024 * 1024
+            collective_id=0, has_side_effects=True, vmem_limit_bytes=40 * 1024 * 1024
         ),
     )(
-        hidden_in[0], attn_gain[None], *tables, post_gain[None],
-        w_query, w_keyval, w_output,
+        *(pltpu.with_memory_space_constraint(a, pltpu.HBM) for a in operands)
     )
     return result[None]
 

time: 64.7 us -> 61.2 us (0.946)
  Pallas kernels: 62.9 us -> 60.3 us
  local copies, waits for them, and re-layouts: 1.67 us -> 0.71 us
    pallas_call x1, Pallas kernels: 62.9 us -> 60.3 us  [local(): pl.pallas_call(ring_kernel, out_shape=jax.ShapeDtypeStruct((count, width)...]
    unnamed x1, local copies, waits for them, and re-layouts: 1.67 us -> 0.71 us
where the time goes in v3:
time: 61.2 us; the launch traced here: 61.1 us
  Pallas kernels  60.3 us (99%)
  local copies, waits for them, and re-layouts  0.71 us (1%)
    pallas_call x1, Pallas kernels, local(): pl.pallas_call(ring_kernel, out_shape=jax.ShapeDtypeStruct((count, width)...  60.3 us

profile of v3, /device:TPU:1, one launch (start us, length us, event | category | flops | bytes accessed | tf_op | source)
XLA Modules:
  0.0 61.1 jit_solution(4944798763337445016)
XLA Ops:
  0.0 60.3 %shard_map.100 = bf16[64,2048]{1,0:T(8,128)(2,1)S(1)} custom-call(bf16[64,2048]{1,0:T(8,128)(2,1)} %bitcast.5, f32[1,2048]{1,0:T(1,128)} %bitcast.6, f32[128,128]{1,0:T(8,128)} %constant.8.clone.crow_in, f32[128,128]{1,0:T(8,128)} %constant.9.clone.srow_in, f32[32,128]{1,0:T(8,128)} %constant.10.clone.cbase_in, f32[32,128]{1,0:T(8,128)} %constant.11.clone.sbase_in, ...), custom_call_target="tpu_custom_call" | custom-call | tf_op jit(solution)/shard_map/pallas_call | solution.py:451
  60.3 0.7 %copy.12 = bf16[1,64,2048]{2,1,0:T(8,128)(2,1)} copy(bf16[1,64,2048]{2,1,0:T(8,128)(2,1)S(1)} %bitcast.4) | data formatting | bytes 524288

commit v4 on v3

--- a/solution.py
+++ b/solution.py
@@ -17,13 +17,12 @@
 NZ = 16
 HALF = NZ // 2
 PIECES = 4
-PIECE = 2 * ROWS // PIECES
 MESH = pl.DeviceIdType.MESH
 
 
 def ring_kernel(
     hid_in, gain_in, crow_in, srow_in, cbase_in, sbase_in, pgain_in, wq, wkv, wo, out,
-    hid, gain, crow, srow, cbase, sbase, pgain, wbuf, kvbuf, nrel, qbuf, qout, acc, mrow, lrow, proj, cos, sin,
+    hid, gain, crow, srow, cbase, sbase, pgain, wbuf, kvbuf, nrel, qbuf, qout, acc, mrow, lrow, proj, cos, sin, ebuf, sbuf,
     lsem, wss, wcs, wrs, wrc, krs, kss, xss, xrs, css, crs, nss, nrs, qss, qrs,
 ):
     dp = lax.axis_index("dp")
@@ -104,11 +103,17 @@
             wss.at[0], wrs.at[ch, kind], peer,
         ).start()
 
-    def step0(ch):
+    def own_y(ch):
         wcopy(ch, 0, 0, 1, every, yp)
         wcopy(ch, 0, 0, 2, every, ym)
+
+    def own_x(ch):
         wcopy(ch, 2, 0, 4, top, xp)
         wcopy(ch, 2, 0, 4, bottom, xm)
+
+    def step0(ch):
+        own_y(ch)
+        own_x(ch)
 
     def step1(ch):
         awaited(wbuf.at[ch, pl.ds(1, 2)], wrs.at[ch, 0])
@@ -218,21 +223,26 @@
         qout[h] = q[ROWS:]
         remote(qout.at[h], qbuf.at[h], qss.at[0], qrs.at[0], co).start()
 
-    def attend(g):
-        online(kvbuf[g].reshape(8 * ROWS, 2 * HD))
-
-    def attend_way(way):
-        online(
+    def group(g):
+        return tuple(
+            kvbuf[g, :, 2 * i : 2 * i + 2].reshape(8 * ROWS, HD) for i in range(2)
+        )
+
+    def group_way(way):
+        return tuple(
             jnp.concatenate(
-                [kvbuf[0, 2 * ab + way].reshape(2 * ROWS, 2 * HD) for ab in range(2)]
+                [
+                    kvbuf[0, 2 * ab + way, 2 * i : 2 * i + 2].reshape(2 * ROWS, HD)
+                    for ab in range(2)
+                ]
             )
-        )
-
-    def online(kv):
-        keys, values = kv[:, :HD], kv[:, HD:]
+            for i in range(2)
+        )
+
+    def weigh(kv):
         q = qbuf[...].reshape(HEADS * ROWS, HD)
         s = lax.dot_general(
-            q, keys, (((1,), (1,)), ((), ())), preferred_element_type=F32
+            q, kv[0], (((1,), (1,)), ((), ())), preferred_element_type=F32
         )
         old = mrow[:, :1]
         new = jnp.maximum(old, jnp.max(s, axis=1, keepdims=True))
@@ -240,9 +250,34 @@
         e = jnp.exp(s - new)
         lrow[...] = lrow[...] * scale + jnp.sum(e, axis=1, keepdims=True)
         mrow[...] = jnp.broadcast_to(new, mrow.shape)
+        return e.astype(BF16), scale
+
+    def gather(e, scale, kv):
         acc[...] = acc[...] * scale + jnp.dot(
-            e.astype(BF16), values, preferred_element_type=F32
-        )
+            e, kv[1], preferred_element_type=F32
+        )
+
+    def online(kv):
+        e, scale = weigh(kv)
+        gather(e, scale, kv)
+
+    def attend(g):
+        online(group(g))
+
+    def attend_way(way):
+        online(group_way(way))
+
+    def halves(kv):
+        def early():
+            e, scale = weigh(kv())
+            ebuf[:, : e.shape[1]] = e
+            sbuf[...] = jnp.broadcast_to(scale, sbuf.shape)
+
+        def late():
+            v = kv()
+            gather(ebuf[:, : v[1].shape[0]], sbuf[:, :1], v)
+
+        return early, late
 
     def finish():
         att = (acc[...] / lrow[:, :1]).astype(BF16)
@@ -268,39 +303,36 @@
         step0(0)
         step0(1)
         normalize()
+        give_rows()
         step1(0)
-        give_rows()
         step1(1)
         step2(0)
         step2(1)
         partner_rows()
         step3(0)
-        k = rotary(projected(0)).astype(BF16)
-        kvbuf[0, 0, :, :, :HD] = k.reshape(PIECES, PIECE, HD)
-
-        def first(cols):
-            for half in range(PIECES):
+        def first(part, u):
+            kvbuf[0, 0, 2 * part : 2 * part + 2] = u.astype(BF16).reshape(2, ROWS, HD)
+            for half in range(2 * part, 2 * part + 2):
                 remote(
-                    kvbuf.at[0, 0, half, :, cols], kvbuf.at[0, 2, half, :, cols],
+                    kvbuf.at[0, 0, half], kvbuf.at[0, 2, half],
                     xss.at[0], xrs.at[half], xo,
                 ).start()
-                for way, peer in ((0, zp), (1, zm)):
-                    remote(
-                        kvbuf.at[0, 0, half, :, cols], kvbuf.at[1, way, half, :, cols],
-                        kss.at[0], krs.at[1, 0, half], peer,
-                    ).start()
-
-        first(pl.ds(0, HD))
+                hops(1, 0, half, True)
+
+        first(0, rotary(projected(0)))
         step3(1)
-        v = projected(1).astype(BF16)
-        kvbuf[0, 0, :, :, HD:] = v.reshape(PIECES, PIECE, HD)
-        first(pl.ds(HD, HD))
+        first(1, projected(1))
         cross(0, 0, 0).start()
 
-        def turn(s, ab):
+        def between(half, work):
+            if work and half % (PIECES // 2) == PIECES // 2 - 1:
+                work[half // (PIECES // 2)]()
+
+        def turn(s, ab, work=None):
             for half in range(PIECES):
                 landed(s - 1, ab, half)
                 hops(s, ab, half)
+                between(half, work)
 
         turn(2, 0)
         for half in range(PIECES):
@@ -319,25 +351,26 @@
         turn(6, 0)
         turn(5, 1)
         cross(4, pl.ds(0, 4), 0).start()
+        turn(7, 0)
         awaited(qbuf, qrs.at[0])
-        attend_way(0)
-        attend(1)
-        turn(7, 0)
-        attend(2)
-        turn(6, 1)
+        turn(6, 1, halves(lambda: group(1)))
         cross(5, pl.ds(0, 4), 0).start()
-        attend(3)
+        work = halves(lambda: group(2))
         for half in range(PIECES):
             landed(HALF - 1, 0, half)
-            hop((HALF - 1, 0), (0, 1), half, zp)
-        attend(4)
-        turn(7, 1)
+            hop((HALF - 1, half % 2), (0, 1), half, (zp, zm)[half % 2])
+            between(half, work)
+        cross(HALF - 1, pl.ds(0, 2), 0).start()
+        turn(7, 1, halves(lambda: group(3)))
         cross(6, pl.ds(0, 4), 0).start()
-        attend(5)
+        work = halves(lambda: group(4))
         for half in range(PIECES):
             landed(HALF - 1, 1, half)
-            hop((HALF - 1, 3), (0, 3), half, zm)
-        cross(HALF - 1, pl.ds(0, 4), 0).start()
+            hop((HALF - 1, 2 + half % 2), (0, 3), half, (zp, zm)[half % 2])
+            between(half, work)
+        cross(HALF - 1, pl.ds(2, 2), 1).start()
+        attend(5)
+        attend_way(0)
         attend(6)
         attend(7)
         for ab in range(2):
@@ -357,7 +390,11 @@
     @pl.when(c == 0)
     def _():
         awaited(wbuf.at[pl.ds(QS, 2 * HEADS), 0], lsem.at[1])
-        step0(2)
+        own_x(2)
+        own_x(3)
+        own_x(4)
+        own_x(5)
+        own_x(6)
         normalize()
         give_rows()
         partner_rows()
@@ -371,12 +408,13 @@
                 awaited(kvbuf.at[0, j], crs.at[0, k])
             attend_way(0)
 
-        step0(3)
-        step0(4)
+        own_y(2)
         step1(2)
-        step0(5)
+        own_y(3)
+        own_y(4)
+        own_y(5)
         step1(3)
-        step0(6)
+        own_y(6)
         xstep1(4)
         step2(2)
         step0(7)
@@ -422,7 +460,9 @@
         near(5)
         near(6)
         give(11)
-        near(7)
+        awaited(kvbuf.at[HALF - 1, pl.ds(0, 2)], crs.at[HALF - 1, 0])
+        awaited(kvbuf.at[HALF - 1, pl.ds(2, 2)], crs.at[HALF - 1, 1])
+        attend(7)
         for j, k in ((1, 2), (3, 3)):
             awaited(kvbuf.at[0, j], crs.at[0, k])
         attend_way(1)
@@ -462,7 +502,7 @@
             pltpu.VMEM((2 * NZ, HD // 2), F32),
             pltpu.VMEM((1, width), F32),
             pltpu.VMEM((NCH, 8, HD, HD), BF16),
-            pltpu.VMEM((HALF, 4, PIECES, PIECE, 2 * HD), BF16),
+            pltpu.VMEM((HALF, 4, PIECES, ROWS, HD), BF16),
             pltpu.VMEM((2 * ROWS, 8 * HD), BF16),
             pltpu.VMEM((HEADS, ROWS, HD), BF16),
             pltpu.VMEM((HEADS, ROWS, HD), BF16),
@@ -472,6 +512,8 @@
             pltpu.VMEM((ROWS, 8 * HD), F32),
             pltpu.VMEM((2 * ROWS, HD // 2), F32),
             pltpu.VMEM((2 * ROWS, HD // 2), F32),
+            pltpu.VMEM((HEADS * ROWS, 8 * ROWS), BF16),
+            pltpu.VMEM((HEADS * ROWS, 128), F32),
             dma((9,)),
             dma((1,)),
             dma((1,)),

time: 61.2 us -> 59.3 us (0.969)
  Pallas kernels: 60.3 us -> 58.5 us
    pallas_call x1, Pallas kernels: 60.3 us -> 58.5 us  [local(): pl.pallas_call(ring_kernel, out_shape=jax.ShapeDtypeStruct((count, width)...]
where the time goes in v4:
time: 59.3 us; the launch traced here: 59.2 us
  Pallas kernels  58.5 us (99%)
  local copies, waits for them, and re-layouts  0.71 us (1%)
    pallas_call x1, Pallas kernels, local(): pl.pallas_call(ring_kernel, out_shape=jax.ShapeDtypeStruct((count, width)...  58.5 us

profile of v4, /device:TPU:1, one launch (start us, length us, event | category | flops | bytes accessed | tf_op | source)
XLA Modules:
  0.0 59.2 jit_solution(7948252947112486286)
XLA Ops:
  0.0 58.5 %shard_map.100 = bf16[64,2048]{1,0:T(8,128)(2,1)S(1)} custom-call(bf16[64,2048]{1,0:T(8,128)(2,1)} %bitcast.5, f32[1,2048]{1,0:T(1,128)} %bitcast.6, f32[128,128]{1,0:T(8,128)} %constant.8.clone.crow_in, f32[128,128]{1,0:T(8,128)} %constant.9.clone.srow_in, f32[32,128]{1,0:T(8,128)} %constant.10.clone.cbase_in, f32[32,128]{1,0:T(8,128)} %constant.11.clone.sbase_in, ...), custom_call_target="tpu_custom_call" | custom-call | tf_op jit(solution)/shard_map/pallas_call | solution.py:491
  58.5 0.7 %copy.12 = bf16[1,64,2048]{2,1,0:T(8,128)(2,1)} copy(bf16[1,64,2048]{2,1,0:T(8,128)(2,1)S(1)} %bitcast.4) | data formatting | bytes 524288

commit v5 on v4

--- a/solution.py
+++ b/solution.py
@@ -114,6 +114,24 @@
     def step0(ch):
         own_y(ch)
         own_x(ch)
+
+    def first0(ch):
+        for kind, up, down in ((0, top, bottom), (5, bottom, top)):
+            wcopy(ch, kind, 0, 1, up, yp)
+            wcopy(ch, kind, 0, 2, down, ym)
+        own_x(ch)
+
+    def first1(ch):
+        awaited(wbuf.at[ch, 1], wrs.at[ch, 0])
+        wcopy(ch, 1, 1, 3, top, yp)
+        wcopy(ch, 1, 2, 3, bottom, ym)
+        wcopy(ch, 2, 1, 5, top, xp)
+        wcopy(ch, 2, 2, 6, bottom, xm)
+
+    def second1(ch):
+        awaited(wbuf.at[ch, 2], wrs.at[ch, 5])
+        wcopy(ch, 2, 2, 6, top, xp)
+        wcopy(ch, 2, 1, 5, bottom, xm)
 
     def step1(ch):
         awaited(wbuf.at[ch, pl.ds(1, 2)], wrs.at[ch, 0])
@@ -280,15 +298,14 @@
         return early, late
 
     def finish():
-        att = (acc[...] / lrow[:, :1]).astype(BF16)
+        heads = (acc[...] / lrow[:, :1]).astype(BF16)
+        att = jnp.concatenate(
+            [heads[h * ROWS : (h + 1) * ROWS] for h in range(HEADS)], axis=1
+        )
         total = jnp.zeros((ROWS, 1), F32)
         for slot in range(8):
-            part = jnp.zeros((ROWS, HD), F32)
-            for h in range(HEADS):
-                part += jnp.dot(
-                    att[h * ROWS : (h + 1) * ROWS], wbuf[OS + h, slot],
-                    preferred_element_type=F32,
-                )
+            w = wbuf[OS:, slot].reshape(HEADS * HD, HD)
+            part = jnp.dot(att, w, preferred_element_type=F32)
             proj[:, slot * HD : (slot + 1) * HD] = part
             total += jnp.sum(part * part, axis=1, keepdims=True)
         inv = lax.rsqrt(total / (8 * HD) + 1e-06)
@@ -300,12 +317,14 @@
     @pl.when(c == 1)
     def _():
         awaited(wbuf.at[pl.ds(0, 2), 0], lsem.at[0])
-        step0(0)
-        step0(1)
+        first0(0)
+        first0(1)
         normalize()
         give_rows()
-        step1(0)
-        step1(1)
+        first1(0)
+        second1(0)
+        first1(1)
+        second1(1)
         step2(0)
         step2(1)
         partner_rows()
@@ -517,7 +536,7 @@
             dma((9,)),
             dma((1,)),
             dma((1,)),
-            dma((NCH, 5)),
+            dma((NCH, 6)),
             dma((HEADS,)),
             dma((HALF, 2, PIECES)),
             dma((1,)),

time: 59.3 us -> 59.4 us (level)
  no operation moved by 1% of the time
where the time goes in v5:
time: 59.4 us; the launch traced here: 59.3 us
  Pallas kernels  58.6 us (99%)
  local copies, waits for them, and re-layouts  0.71 us (1%)
    pallas_call x1, Pallas kernels, local(): pl.pallas_call(ring_kernel, out_shape=jax.ShapeDtypeStruct((count, width)...  58.6 us

profile of v5, /device:TPU:1, one launch (start us, length us, event | category | flops | bytes accessed | tf_op | source)
XLA Modules:
  0.0 59.3 jit_solution(5553809415181214858)
XLA Ops:
  0.0 58.6 %shard_map.100 = bf16[64,2048]{1,0:T(8,128)(2,1)S(1)} custom-call(bf16[64,2048]{1,0:T(8,128)(2,1)} %bitcast.5, f32[1,2048]{1,0:T(1,128)} %bitcast.6, f32[128,128]{1,0:T(8,128)} %constant.8.clone.crow_in, f32[128,128]{1,0:T(8,128)} %constant.9.clone.srow_in, f32[32,128]{1,0:T(8,128)} %constant.10.clone.cbase_in, f32[32,128]{1,0:T(8,128)} %constant.11.clone.sbase_in, ...), custom_call_target="tpu_custom_call" | custom-call | tf_op jit(solution)/shard_map/pallas_call | solution.py:510
  58.6 0.7 %copy.12 = bf16[1,64,2048]{2,1,0:T(8,128)(2,1)} copy(bf16[1,64,2048]{2,1,0:T(8,128)(2,1)S(1)} %bitcast.4) | data formatting | bytes 524288
